TPU v7x, 32 devices: a whole 2x2x4 slice. The times are simulated.
32 devices in a mesh: mom: 8 (over y, x, core), en: 4 (over z).
Axes of the slice: x: 2, y: 2, z: 4, core: 2. Of those that a mesh axis runs over, the one named last changes fastest.
Arguments:
- green: bfloat16 [2, 8, 16, 2, 128, 128], P(None, 'mom', 'en'), may hold values from -0.5 to 0.5
- bare: bfloat16 [2, 8, 16, 2, 128, 128], P(None, 'mom', 'en'), may hold values from -0.5 to 0.5
- coupling: bfloat16 [4, 128, 128], replicated, may hold values from -0.25 to 0.25
- occupation: float32 [4], replicated, may hold values from 0.2 to 2
- mode_shift: int32 [4], replicated, may hold values from -1 to 1, as said below
- mode_offset: int32 [4], replicated, may hold values from 1 to 4, as said below
- mode_block: int32 [2, 4], replicated, may hold values from 0 to 1
Outputs:
- updated: bfloat16 [2, 8, 16, 2, 128, 128], P(None, 'mom', 'en')
Inputs may be any that keep to these rules, and one draw needn't show every extreme that they name: `mode_shift`: each of -1, 0 and 1 is the shift of some mode. `mode_offset`: every offset from 1 to 4 is some mode's.
All inputs are finite; a program needn't handle non-finite values.
Results may differ from a plain program's by a relative error of at most 0.02.
Values may be sent and summed in bfloat16 or wider, within the bound.
A program may use at most 64 MiB of HBM per device.

v0:
```python
import jax
import jax.numpy as jnp
from jax import lax
from jax.sharding import PartitionSpec as P

MODES = 4
REACH = 4
PASSES = 2


def extended(block, sides, width):
    for axis, dim in sides:
        count = lax.axis_size(axis)
        forward = [(i, i + 1) for i in range(count - 1)]
        backward = [(target, source) for source, target in forward]
        low = lax.ppermute(
            lax.slice_in_dim(block, block.shape[dim] - width, None, axis=dim), axis, forward
        )
        high = lax.ppermute(lax.slice_in_dim(block, 0, width, axis=dim), axis, backward)
        block = jnp.concatenate([low, block, high], axis=dim)
    return block


def shifted(array, axis, by):
    size = lax.axis_size(axis)
    return lax.ppermute(array, axis, [(i, (i + by) % size) for i in range(size)])


def product_of(left_part, right_part):
    return jnp.einsum(
        "...ab,...bc->...ac", left_part, right_part, preferred_element_type=jnp.float32
    )


def complex_product(left_pair, right_pair):
    real_part = product_of(left_pair[0], right_pair[0]) - product_of(left_pair[1], right_pair[1])
    imag_part = product_of(left_pair[0], right_pair[1]) + product_of(left_pair[1], right_pair[0])
    return jnp.stack([real_part, imag_part])


def mode_term(stacked, which, coupling, occupation, mode_offset, mode_block, mode_index, energies):
    source = lax.dynamic_index_in_dim(stacked, which, 0, keepdims=False)
    weight = occupation[mode_index]
    lower_start = REACH - mode_offset[mode_index]
    upper_start = REACH + mode_offset[mode_index]
    pieces = []
    for target in range(source.shape[3]):
        picked = lax.dynamic_index_in_dim(source, mode_block[target, mode_index], 3, keepdims=True)
        lower_side = lax.dynamic_slice_in_dim(picked, lower_start, energies, 2)
        upper_side = lax.dynamic_slice_in_dim(picked, upper_start, energies, 2)
        mixed = weight * lower_side.astype(jnp.float32) + (weight + 1.0) * upper_side.astype(
            jnp.float32
        )
        pieces.append(mixed.astype(jnp.bfloat16))
    summed = jnp.concatenate(pieces, axis=3)
    matrix = coupling[mode_index]
    coupled = jnp.einsum(
        "ab,...bc->...ac", matrix, summed, preferred_element_type=jnp.float32
    ).astype(jnp.bfloat16)
    return jnp.einsum("...ab,cb->...ac", coupled, matrix, preferred_element_type=jnp.float32)


def shares_by_shift(rimmed, coupling, occupation, mode_shift, mode_offset, mode_block, energies):
    stacked = rimmed[None]
    shape = (3, 2, 1, energies) + rimmed.shape[3:]
    shares = jnp.zeros(shape, jnp.float32)
    for mode_index in range(MODES):
        term = mode_term(
            stacked, 0, coupling, occupation, mode_offset, mode_block, mode_index, energies
        )
        which = mode_shift[mode_index] + 1
        previous = lax.dynamic_index_in_dim(shares, which, 0, keepdims=False)
        shares = lax.dynamic_update_index_in_dim(shares, previous + term, which, 0)
    return shares


def shards(green, bare, coupling, occupation, mode_shift, mode_offset, mode_block):
    energies = green.shape[2]
    current = green
    for pass_index in range(PASSES):
        rimmed = extended(current, (("en", 2),), REACH)
        shares = shares_by_shift(
            rimmed, coupling, occupation, mode_shift, mode_offset, mode_block, energies
        )
        total = shares[1]
        for towards, outgoing in ((-1, shares[0]), (1, shares[2])):
            total = total + shifted(outgoing.astype(jnp.bfloat16), "mom", towards).astype(
                outgoing.dtype
            )
        sigma = total.astype(jnp.bfloat16)
        product = complex_product(bare, sigma).astype(jnp.bfloat16)
        correction = complex_product(product, bare)
        current = (bare.astype(jnp.float32) + correction).astype(jnp.bfloat16)
    return current


def solution(mesh):
    placed = (
        P(None, "mom", "en", None, None, None),
        P(None, "mom", "en", None, None, None),
        P(),
        P(),
        P(),
        P(),
        P(),
    )
    return jax.shard_map(
        shards,
        mesh=mesh,
        in_specs=placed,
        out_specs=P(None, "mom", "en", None, None, None),
        check_vma=False,
    )
```

profile of v0, /device:TPU:0, one launch (start us, length us, event | category | flops | bytes accessed | tf_op | source)
XLA Modules:
  0.0 148.0 jit_solution(581547405150834672)
XLA Ops:
  0.0 1.3 copy.9
  1.3 1.3 collective-permute-start.1
  2.6 5.6 %collective-permute-start = (bf16[2,1,4,2,128,128]{4,5,3,2,0,1:T(8,128)(2,1)S(1)}, bf16[2,1,4,2,128,128]{4,5,3,2,0,1:T(8,128)(2,1)S(1)}, u32[]{:S(2)}, u32[]{:S(2)}) collective-permute-start(bf16[2,1,4,2,128,128]{4,5,3,2,0,1:T(8,128)(2,1)S(1)} %copy.9), channel_id=1, source_target_pairs={{0,1},{1,2},{2,3},{4,5},{5,6},{6,7},{8,9},{9,10},{10,11},{12,13},{... | collective-permute-start | bytes 1572872 | tf_op jit(solution)/shard_map/ppermute | solution.py:16
  8.2 1.5 fusion.159
  14.9 1.5 fusion.158
  26.4 1.6 %fusion.156 = (s32[1,1]{1,0:T(1,128)}, s32[1,1]{1,0:T(1,128)}, s32[1,1]{1,0:T(1,128)}, s32[1,1]{1,0:T(1,128)}, s32[1,1]{1,0:T(1,128)}, /*index=5*/s32[1,1]{1,0:T(1,128)}, s32[1,1]{1,0:T(1,128)}, s32[1,1]{1,0:T(1,128)}) fusion(s32[2,4]{1,0:T(2,128)} %param.13), kind=kLoop, calls=%fused_computation.187 | loop fusion | bytes 64 | tf_op jit(solution)/shard_map/slice | solution.py:48
  38.0 1.5 fusion.157
  47.3 0.9 add_convert_fusion.15
  48.2 2.0 %broadcast.10.clone = f32[3,2,1,4,2,128,128]{5,6,4,3,1,2,0:T(8,128)} broadcast(f32[]{:T(128)} %constant.999.clone.1), dimensions={} | broadcast | bytes 3145732 | tf_op jit(solution)/shard_map/broadcast.1
  50.2 1.6 %fusion = f32[3,2,1,4,2,128,128]{5,6,4,3,1,2,0:T(8,128)} fusion(f32[3,2,1,4,2,128,128]{5,6,4,3,1,2,0:T(8,128)} %broadcast.10.clone, s32[]{:T(128)S(6)} %select_n.156, bf16[2,1,4,1,128,128]{4,5,3,2,0,1:T(8,128)(2,1)S(1)} %get-tuple-element.24, bf16[2,1,4,1,128,128]{4,5,3,2,0,1:T(8,128)(2,1)S(1)} %get-tuple-element.23, bf16[4,128,128]{2,1,0:T(8,128)(2,1)S(1)} %copy-done.2), kind=kOutput, calls=%fused_computation.3 | convolution fusion | flops 134742016 | bytes 1638404 | tf_op jit(solution)/shard_map/...ab,cb->...ac/dot_general | solution.py:60
  51.8 1.3 constant_dynamic-slice_fusion.5
  53.1 1.3 copy.14
  54.4 3.5 %add_convert_fusion.9 = (bf16[2,1,4,1,128,128]{4,5,3,2,0,1:T(8,128)(2,1)S(1)}, bf16[2,1,4,1,128,128]{4,5,3,2,0,1:T(8,128)(2,1)S(1)}, bf16[2,1,4,1,128,128]{4,5,3...) fusion(bf16[2,1,12,2,128,128]{4,5,3,2,0,1:T(8,128)(2,1)S(1)} %p, ...), kind=kLoop, calls=%fused_computation.103 | loop fusion | flops 4718592 | bytes 4718664 | tf_op jit(solution)/shard_map/convert_element_type | solution.py:54
  58.0 1.6 %fusion.10 = f32[1,2,1,4,2,128,128]{6,5,4,3,1,2,0:T(8,128)} fusion(f32[1,2,1,4,2,128,128]{6,5,4,3,1,2,0:T(8,128)S(1)} %copy-done.1, bf16[2,1,4,1,128,128]{4,5,3,2,0,1:T(8,128)(2,1)S(1)} %get-tuple-element.18, bf16[2,1,4,1,128,128]{4,5,3,2,0,1:T(8,128)(2,1)S(1)} %get-tuple-element.20, bf16[4,128,128]{2,1,0:T(8,128)(2,1)S(1)} %copy-done.2), kind=kOutput, calls=%fused_computation.20 | convolution fusion | flops 135004160 | bytes 2686976 | tf_op jit(solution)/shard_map/...ab,cb->...ac/dot_general | solution.py:60
  59.5 1.6 %copy.16 = f32[1,2,1,4,2,128,128]{5,6,4,3,1,2,0:T(8,128)S(1)} copy(f32[1,2,1,4,2,128,128]{6,5,4,3,1,2,0:T(8,128)} %fusion.10) | data formatting | bytes 2097152 | tf_op jit(solution)/shard_map/jit(dynamic_update_index_in_dim)/broadcast_in_dim | solution.py:73
  61.1 1.1 constant_dynamic-update-slice_fusion.2
  62.2 1.3 constant_dynamic-slice_fusion.4
  63.5 0.3 copy.17
  63.8 1.6 %fusion.9 = f32[1,2,1,4,2,128,128]{6,5,4,3,1,2,0:T(8,128)S(1)} fusion(f32[1,2,1,4,2,128,128]{6,5,4,3,1,2,0:T(8,128)S(1)} %copy.17, bf16[2,1,4,1,128,128]{4,5,3,2,0,1:T(8,128)(2,1)} %get-tuple-element.19, bf16[2,1,4,1,128,128]{4,5,3,2,0,1:T(8,128)(2,1)} %get-tuple-element.21, bf16[4,128,128]{2,1,0:T(8,128)(2,1)S(1)} %copy-done.2), kind=kOutput, calls=%fused_computation.18 | convolution fusion | flops 135004160 | bytes 2686976 | tf_op jit(solution)/shard_map/...ab,cb->...ac/dot_general | solution.py:60
  65.4 0.3 copy.19
  65.8 1.1 constant_dynamic-update-slice_fusion.1
  66.8 1.3 constant_dynamic-slice_fusion.2
  68.1 0.3 copy.20
  68.5 0.6 fusion.8
  69.1 0.3 copy.22
  69.4 1.1 constant_dynamic-update-slice_fusion
  70.5 2.2 %convert.28 = bf16[3,2,1,4,2,128,128]{5,6,4,3,1,2,0:T(8,128)(2,1)S(1)} convert(f32[3,2,1,4,2,128,128]{5,6,4,3,1,2,0:T(8,128)} %constant_dynamic-update-slice_fusion) | non-fusion elementwise | flops 786432 | bytes 4718592 | tf_op jit(solution)/shard_map/convert.15
  72.8 1.8 %collective-permute-start.2 = (bf16[2,1,4,2,128,128]{4,5,3,2,0,1:T(8,128)(2,1)S(1)}, bf16[2,1,4,2,128,128]{4,5,3,2,0,1:T(8,128)(2,1)S(1)}, u32[]{:S(2)}, u32[]{:S(2)}) collective-permute-start(bf16[2,1,4,2,128,128]{4,5,3,2,0,1:T(8,128)(2,1)S(1)} %get-tuple-element.15), channel_id=1, source_target_pairs={{0,28},{4,0},{8,4},{12,8},{16,12},{20,16},{24,20},{28,24},{1,29},{... | collective-permute-start | bytes 1572872 | tf_op jit(solution)/shard_map/ppermute | solution.py:26
  74.6 0.3 copy.8
  74.9 11.7 %collective-permute-done.2 = bf16[2,1,4,2,128,128]{4,5,3,2,0,1:T(8,128)(2,1)S(1)} collective-permute-done((bf16[2,1,4,2,128,128]{4,5,3,2,0,1:T(8,128)(2,1)S(1)}, bf16[2,1,4,2,128,128]{4,5,3,2,0,1:T(8,128)(2,1)S(1)}, u32[]{:S(2)}, u32[]{:S(2)}) %collective-permute-start.2) | collective-permute-done | bytes 524320 | tf_op jit(solution)/shard_map/ppermute | solution.py:26
  86.6 1.9 %collective-permute-done.3 = bf16[2,1,4,2,128,128]{4,5,3,2,1,0:T(8,128)(2,1)S(1)} collective-permute-done((bf16[2,1,4,2,128,128]{4,5,3,2,1,0:T(8,128)(2,1)S(1)}, bf16[2,1,4,2,128,128]{4,5,3,2,1,0:T(8,128)(2,1)S(1)}, u32[]{:S(2)}, u32[]{:S(2)}) %collective-permute-start.3) | collective-permute-done | bytes 524320 | tf_op jit(solution)/shard_map/ppermute | solution.py:26
  88.5 1.4 fusion.35
  89.9 0.3 fusion.86
  90.2 0.3 fusion.90
  90.5 0.3 fusion.23
  91.4 0.3 fusion.24
  91.7 0.3 fusion.22
  92.4 1.3 collective-permute-start.5
  93.7 4.8 %collective-permute-start.4 = (bf16[2,1,4,2,128,128]{4,5,3,2,0,1:T(8,128)(2,1)S(1)}, bf16[2,1,4,2,128,128]{4,5,3,2,0,1:T(8,128)(2,1)S(1)}, u32[]{:S(2)}, u32[]{:S(2)}) collective-permute-start(bf16[2,1,4,2,128,128]{4,5,3,2,0,1:T(8,128)(2,1)S(1)} %fusion.27), channel_id=1, source_target_pairs={{0,1},{1,2},{2,3},{4,5},{5,6},{6,7},{8,9},{9,10},{10,11},{12,13},{... | collective-permute-start | bytes 1572872 | tf_op jit(solution)/shard_map/ppermute | solution.py:16
  98.5 7.6 %collective-permute-done.5 = bf16[2,1,4,2,128,128]{4,5,3,2,0,1:T(8,128)(2,1)S(1)} collective-permute-done((bf16[2,1,4,2,128,128]{4,5,3,2,0,1:T(8,128)(2,1)S(1)}, bf16[2,1,4,2,128,128]{4,5,3,2,0,1:T(8,128)(2,1)S(1)}, u32[]{:S(2)}, u32[]{:S(2)}) %collective-permute-start.5) | collective-permute-done | bytes 524320 | tf_op jit(solution)/shard_map/ppermute | solution.py:19
  106.1 1.2 collective-permute-done.4
  107.4 0.8 add_convert_fusion.7
  108.3 3.2 %add_convert_fusion.1 = (bf16[2,1,4,1,128,128]{4,5,3,2,0,1:T(8,128)(2,1)S(1)}, bf16[2,1,4,1,128,128]{4,5,3,2,0,1:T(8,128)(2,1)S(1)}, bf16[2,1,4,1,128,128]{4,5,3...) fusion(bf16[2,1,12,2,128,128]{4,5,3,2,0,1:T(8,128)(2,1)S(1)} %p, ...), kind=kLoop, calls=%fused_computation.95 | loop fusion | flops 4718592 | bytes 4718664 | tf_op jit(solution)/shard_map/convert_element_type | solution.py:54
  111.5 2.0 %broadcast.10 = f32[3,2,1,4,2,128,128]{5,6,4,3,1,2,0:T(8,128)} broadcast(f32[]{:T(128)} %constant.999.clone.1), dimensions={} | broadcast | bytes 3145732 | tf_op jit(solution)/shard_map/broadcast.1
  113.6 1.6 %fusion.1 = f32[3,2,1,4,2,128,128]{5,6,4,3,1,2,0:T(8,128)} fusion(f32[3,2,1,4,2,128,128]{5,6,4,3,1,2,0:T(8,128)} %broadcast.10, s32[]{:T(128)S(6)} %select_n.156, bf16[2,1,4,1,128,128]{4,5,3,2,0,1:T(8,128)(2,1)S(1)} %get-tuple-element.14, bf16[2,1,4,1,128,128]{4,5,3,2,0,1:T(8,128)(2,1)S(1)} %get-tuple-element.13, bf16[4,128,128]{2,1,0:T(8,128)(2,1)S(1)} %copy-done.2), kind=kOutput, calls=%fused_computation.5 | convolution fusion | flops 134742016 | bytes 1638404 | tf_op jit(solution)/shard_map/...ab,cb->...ac/dot_general | solution.py:60
  115.1 1.3 constant_dynamic-slice_fusion.1
  116.4 2.5 %fusion.7 = f32[3,2,1,4,2,128,128]{5,6,4,3,1,2,0:T(8,128)} fusion(f32[3,2,1,4,2,128,128]{5,6,4,3,1,2,0:T(8,128)} %fusion.1, s32[]{:T(128)S(6)} %select_n.157, f32[1,2,1,4,2,128,128]{5,6,4,3,1,2,0:T(8,128)S(1)} %constant_dynamic-slice_fusion.1, bf16[2,1,4,1,128,128]{4,5,3,2,0,1:T(8,128)(2,1)S(1)} %get-tuple-element.8, ...), kind=kOutput, calls=%fused_computation.14 | convolution fusion | flops 135004160 | bytes 2686980 | tf_op jit(solution)/shard_map/...ab,cb->...ac/dot_general | solution.py:60
  118.9 1.3 constant_dynamic-slice_fusion.3
  120.2 1.6 %fusion.5 = f32[3,2,1,4,2,128,128]{5,6,4,3,1,2,0:T(8,128)} fusion(f32[3,2,1,4,2,128,128]{5,6,4,3,1,2,0:T(8,128)} %fusion.7, s32[]{:T(128)S(6)} %select_n.166, f32[1,2,1,4,2,128,128]{5,6,4,3,1,2,0:T(8,128)S(1)} %constant_dynamic-slice_fusion.3, bf16[2,1,4,1,128,128]{4,5,3,2,0,1:T(8,128)(2,1)S(1)} %get-tuple-element.9, ...), kind=kOutput, calls=%fused_computation.11 | convolution fusion | flops 135004160 | bytes 2686980 | tf_op jit(solution)/shard_map/...ab,cb->...ac/dot_general | solution.py:60
  121.8 1.3 constant_dynamic-slice_fusion
  123.1 1.6 %fusion.3 = f32[3,2,1,4,2,128,128]{5,6,4,3,1,2,0:T(8,128)} fusion(f32[3,2,1,4,2,128,128]{5,6,4,3,1,2,0:T(8,128)} %fusion.5, s32[]{:T(128)S(6)} %select_n.175, f32[1,2,1,4,2,128,128]{5,6,4,3,1,2,0:T(8,128)S(1)} %constant_dynamic-slice_fusion, bf16[2,1,4,1,128,128]{4,5,3,2,0,1:T(8,128)(2,1)S(1)} %get-tuple-element.12, ...), kind=kOutput, calls=%fused_computation.8 | convolution fusion | flops 135004160 | bytes 2686980 | tf_op jit(solution)/shard_map/...ab,cb->...ac/dot_general | solution.py:60
  124.7 2.1 %convert.31 = bf16[3,2,1,4,2,128,128]{5,6,4,3,1,2,0:T(8,128)(2,1)S(1)} convert(f32[3,2,1,4,2,128,128]{5,6,4,3,1,2,0:T(8,128)} %fusion.3) | non-fusion elementwise | flops 786432 | bytes 4718592 | tf_op jit(solution)/shard_map/convert.7
  126.9 2.3 %collective-permute-start.6 = (bf16[2,1,4,2,128,128]{4,5,3,2,0,1:T(8,128)(2,1)S(1)}, bf16[2,1,4,2,128,128]{4,5,3,2,0,1:T(8,128)(2,1)S(1)}, u32[]{:S(2)}, u32[]{:S(2)}) collective-permute-start(bf16[2,1,4,2,128,128]{4,5,3,2,0,1:T(8,128)(2,1)S(1)} %get-tuple-element.5), channel_id=1, source_target_pairs={{0,28},{4,0},{8,4},{12,8},{16,12},{20,16},{24,20},{28,24},{1,29},{... | collective-permute-start | bytes 1572872 | tf_op jit(solution)/shard_map/ppermute | solution.py:26
  129.2 11.6 %collective-permute-done.6 = bf16[2,1,4,2,128,128]{4,5,3,2,0,1:T(8,128)(2,1)S(1)} collective-permute-done((bf16[2,1,4,2,128,128]{4,5,3,2,0,1:T(8,128)(2,1)S(1)}, bf16[2,1,4,2,128,128]{4,5,3,2,0,1:T(8,128)(2,1)S(1)}, u32[]{:S(2)}, u32[]{:S(2)}) %collective-permute-start.6) | collective-permute-done | bytes 524320 | tf_op jit(solution)/shard_map/ppermute | solution.py:26
  140.8 2.3 %collective-permute-done.7 = bf16[2,1,4,2,128,128]{4,5,3,2,0,1:T(8,128)(2,1)S(1)} collective-permute-done((bf16[2,1,4,2,128,128]{4,5,3,2,0,1:T(8,128)(2,1)S(1)}, bf16[2,1,4,2,128,128]{4,5,3,2,0,1:T(8,128)(2,1)S(1)}, u32[]{:S(2)}, u32[]{:S(2)}) %collective-permute-start.7) | collective-permute-done | bytes 524320 | tf_op jit(solution)/shard_map/ppermute | solution.py:26
  143.1 1.4 fusion.31
  144.5 0.3 fusion.79
  144.8 0.3 fusion.83
  145.1 0.3 fusion.25
  145.7 0.3 fusion.68
  146.0 0.3 fusion.26
  146.3 0.3 fusion.20
  146.6 0.3 fusion.19
  147.0 1.0 copy.48
  (22 shorter events, 1.9 us)
Async XLA Ops:
  1.3 45.8 %collective-permute-start.1 = (bf16[2,1,4,2,128,128]{4,5,3,2,0,1:T(8,128)(2,1)S(1)}, bf16[2,1,4,2,128,128]{4,5,3,2,0,1:T(8,128)(2,1)S(1)}, u32[]{:S(2)}, u32[]{:S(2)}) collective-permute-start(bf16[2,1,4,2,128,128]{4,5,3,2,0,1:T(8,128)(2,1)S(1)} %copy.9), channel_id=1, source_target_pairs={{1,0},{2,1},{3,2},{5,4},{6,5},{7,6},{9,8},{10,9},{11,10},{13,12},{... | collective-permute-start | bytes 1572872 | tf_op jit(solution)/shard_map/ppermute | solution.py:19
  2.6 44.5 %collective-permute-start = (bf16[2,1,4,2,128,128]{4,5,3,2,0,1:T(8,128)(2,1)S(1)}, bf16[2,1,4,2,128,128]{4,5,3,2,0,1:T(8,128)(2,1)S(1)}, u32[]{:S(2)}, u32[]{:S(2)}) collective-permute-start(bf16[2,1,4,2,128,128]{4,5,3,2,0,1:T(8,128)(2,1)S(1)} %copy.9), channel_id=1, source_target_pairs={{0,1},{1,2},{2,3},{4,5},{5,6},{6,7},{8,9},{9,10},{10,11},{12,13},{... | collective-permute-start | bytes 1572872 | tf_op jit(solution)/shard_map/ppermute | solution.py:16
  47.3 2.9 %copy-start.2 = (bf16[4,128,128]{2,1,0:T(8,128)(2,1)S(1)}, bf16[4,128,128]{2,1,0:T(8,128)(2,1)}, u32[]{:S(2)}) copy-start(bf16[4,128,128]{2,1,0:T(8,128)(2,1)} %param.9) | copy-start | bytes 393220
  54.4 3.5 %copy-start.1 = (f32[1,2,1,4,2,128,128]{6,5,4,3,1,2,0:T(8,128)S(1)}, f32[1,2,1,4,2,128,128]{6,5,4,3,1,2,0:T(8,128)}, u32[]{:S(2)}) copy-start(f32[1,2,1,4,2,128,128]{6,5,4,3,1,2,0:T(8,128)} %copy.14) | copy-start | bytes 3145732
  65.8 2.7 %copy-start.3 = (bf16[2,1,4,1,128,128]{4,5,3,2,0,1:T(8,128)(2,1)S(1)}, bf16[2,1,4,1,128,128]{4,5,3,2,0,1:T(8,128)(2,1)}, u32[]{:S(2)}) copy-start(bf16[2,1,4,1,128,128]{4,5,3,2,0,1:T(8,128)(2,1)} %get-tuple-element.22) | copy-start | bytes 786436
  70.5 4.1 %copy-start = (bf16[2,1,4,2,128,128]{5,4,3,2,1,0:T(8,128)(2,1)S(1)}, bf16[2,1,4,2,128,128]{5,4,3,2,1,0:T(8,128)(2,1)}, u32[]{:S(2)}) copy-start(bf16[2,1,4,2,128,128]{5,4,3,2,1,0:T(8,128)(2,1)} %param.8) | copy-start | bytes 1572868
  72.8 13.8 %collective-permute-start.2 = (bf16[2,1,4,2,128,128]{4,5,3,2,0,1:T(8,128)(2,1)S(1)}, bf16[2,1,4,2,128,128]{4,5,3,2,0,1:T(8,128)(2,1)S(1)}, u32[]{:S(2)}, u32[]{:S(2)}) collective-permute-start(bf16[2,1,4,2,128,128]{4,5,3,2,0,1:T(8,128)(2,1)S(1)} %get-tuple-element.15), channel_id=1, source_target_pairs={{0,28},{4,0},{8,4},{12,8},{16,12},{20,16},{24,20},{28,24},{1,29},{... | collective-permute-start | bytes 1572872 | tf_op jit(solution)/shard_map/ppermute | solution.py:26
  74.6 13.9 %collective-permute-start.3 = (bf16[2,1,4,2,128,128]{4,5,3,2,1,0:T(8,128)(2,1)S(1)}, bf16[2,1,4,2,128,128]{4,5,3,2,1,0:T(8,128)(2,1)S(1)}, u32[]{:S(2)}, u32[]{:S(2)}) collective-permute-start(bf16[2,1,4,2,128,128]{4,5,3,2,1,0:T(8,128)(2,1)S(1)} %get-tuple-element.16), channel_id=1, source_target_pairs={{0,4},{4,8},{8,12},{12,16},{16,20},{20,24},{24,28},{28,0},{1,5},{5... | collective-permute-start | bytes 1572872 | tf_op jit(solution)/shard_map/ppermute | solution.py:26
  92.4 13.7 %collective-permute-start.5 = (bf16[2,1,4,2,128,128]{4,5,3,2,0,1:T(8,128)(2,1)S(1)}, bf16[2,1,4,2,128,128]{4,5,3,2,0,1:T(8,128)(2,1)S(1)}, u32[]{:S(2)}, u32[]{:S(2)}) collective-permute-start(bf16[2,1,4,2,128,128]{4,5,3,2,0,1:T(8,128)(2,1)S(1)} %fusion.27), channel_id=1, source_target_pairs={{1,0},{2,1},{3,2},{5,4},{6,5},{7,6},{9,8},{10,9},{11,10},{13,12},{... | collective-permute-start | bytes 1572872 | tf_op jit(solution)/shard_map/ppermute | solution.py:19
  93.7 13.5 %collective-permute-start.4 = (bf16[2,1,4,2,128,128]{4,5,3,2,0,1:T(8,128)(2,1)S(1)}, bf16[2,1,4,2,128,128]{4,5,3,2,0,1:T(8,128)(2,1)S(1)}, u32[]{:S(2)}, u32[]{:S(2)}) collective-permute-start(bf16[2,1,4,2,128,128]{4,5,3,2,0,1:T(8,128)(2,1)S(1)} %fusion.27), channel_id=1, source_target_pairs={{0,1},{1,2},{2,3},{4,5},{5,6},{6,7},{8,9},{9,10},{10,11},{12,13},{... | collective-permute-start | bytes 1572872 | tf_op jit(solution)/shard_map/ppermute | solution.py:16
  126.9 13.9 %collective-permute-start.6 = (bf16[2,1,4,2,128,128]{4,5,3,2,0,1:T(8,128)(2,1)S(1)}, bf16[2,1,4,2,128,128]{4,5,3,2,0,1:T(8,128)(2,1)S(1)}, u32[]{:S(2)}, u32[]{:S(2)}) collective-permute-start(bf16[2,1,4,2,128,128]{4,5,3,2,0,1:T(8,128)(2,1)S(1)} %get-tuple-element.5), channel_id=1, source_target_pairs={{0,28},{4,0},{8,4},{12,8},{16,12},{20,16},{24,20},{28,24},{1,29},{... | collective-permute-start | bytes 1572872 | tf_op jit(solution)/shard_map/ppermute | solution.py:26
  129.2 13.9 %collective-permute-start.7 = (bf16[2,1,4,2,128,128]{4,5,3,2,0,1:T(8,128)(2,1)S(1)}, bf16[2,1,4,2,128,128]{4,5,3,2,0,1:T(8,128)(2,1)S(1)}, u32[]{:S(2)}, u32[]{:S(2)}) collective-permute-start(bf16[2,1,4,2,128,128]{4,5,3,2,0,1:T(8,128)(2,1)S(1)} %get-tuple-element.6), channel_id=1, source_target_pairs={{0,4},{4,8},{8,12},{12,16},{16,20},{20,24},{24,28},{28,0},{1,5},{5... | collective-permute-start | bytes 1572872 | tf_op jit(solution)/shard_map/ppermute | solution.py:26
where the time goes:
time: 149 us; the launch traced here: 148 us
  waiting for transfers between devices  36.3 us (24%)
  between operations  33.2 us (22%)
  local copies, waits for them, and re-layouts  28 us (19%)
  matrix products  17.2 us (12%)
  starting transfers between devices  17.1 us (11%)
  other arithmetic  16.3 us (11%)
    ppermute x4, waiting for transfers between devices, shifted(): lax.ppermute(array, axis, [(i, (i + by) % size) for i in range(size)])  27.5 us
    dot_general x8, matrix products, mode_term(): jnp.einsum('...ab,cb->...ac', coupled, matrix, preferred_element_type=jnp...  12.6 us
    ppermute x2, starting transfers between devices, extended(): lax.ppermute(lax.slice_in_dim(block, block.shape[dim] - width, None, axis...  10.4 us
    dynamic_slice x9, local copies, waits for them, and re-layouts, shares_by_shift(): previous = lax.dynamic_index_in_dim(shares, which, 0, keepdims=False)  9.74 us
    convert_element_type x4, other arithmetic, mode_term(): pieces.append(mixed.astype(jnp.bfloat16))  8.51 us
    ppermute x2, waiting for transfers between devices, extended(): lax.ppermute(lax.slice_in_dim(block, 0, width, axis=dim), axis, backward)  7.59 us
    dot_general x16, matrix products, product_of(): jnp.einsum('...ab,...bc->...ac', left_part, right_part, preferred_element...  4.66 us
    another operation x2, other arithmetic  4.34 us
  transfers between devices with their start and end apart: 8, of which 6 were waited for; matrix products, arithmetic and copies ran while one was open for 4% of the time, Pallas kernels for 0%

commit v1 on v0

v1 whole, which is shorter than its diff:
```python
import functools

import jax
import jax.numpy as jnp
from jax import lax
from jax.experimental import pallas as pl
from jax.experimental.pallas import tpu as pltpu
from jax.sharding import PartitionSpec as P

MODES = 4
REACH = 4
PASSES = 2

RAW_UP, RAW_DOWN, RAW_NEXT, RAW_PREV, SHARE_NEXT, SHARE_PREV, PART_UP, PART_DOWN = range(8)
KINDS = 8

f32 = jnp.float32
bf16 = jnp.bfloat16


def matmul(left, right):
    return jnp.dot(left, right, preferred_element_type=f32)


def side_by_side(*parts):
    return parts[0] if len(parts) == 1 else jnp.concatenate(parts, axis=1)


def on_top(*parts):
    return parts[0] if len(parts) == 1 else jnp.concatenate(parts, axis=0)


def kernel(
    mom_count, en_count, passes,
    occupation, mode_shift, mode_offset, mode_block, green, bare, coupling,
    out,
    matrices, matrices_t, pair_t, wide_bare, real_coupled, below, above,
    share_own, part_own, real_current, low_rim, high_rim, imag_source,
    share_out, share_in, part_out, part_in, send_sem, recv_sem,
):
    energies = green.shape[2]
    blocks = green.shape[3]
    size = green.shape[4]
    k = lax.axis_index("mom")
    z = lax.axis_index("en")
    next_k = lax.rem(k + 1, mom_count)
    prev_k = lax.rem(k + mom_count - 1, mom_count)
    up_z = lax.rem(z + 1, en_count)
    down_z = lax.rem(z + en_count - 1, en_count)
    has_up = z < en_count - 1
    has_down = z > 0

    barrier = pltpu.get_barrier_semaphore()
    for other in (next_k, prev_k):
        pl.semaphore_signal(
            barrier, inc=1, device_id={"mom": other}, device_id_type=pl.DeviceIdType.MESH
        )

    @pl.when(has_up)
    def _():
        pl.semaphore_signal(
            barrier, inc=1, device_id={"en": up_z}, device_id_type=pl.DeviceIdType.MESH
        )

    @pl.when(has_down)
    def _():
        pl.semaphore_signal(
            barrier, inc=1, device_id={"en": down_z}, device_id_type=pl.DeviceIdType.MESH
        )

    pl.semaphore_wait(barrier, 2 + has_up.astype(jnp.int32) + has_down.astype(jnp.int32))

    def copy_of(p, kind, e):
        if kind == RAW_UP or kind == RAW_DOWN:
            source = green.at[0, 0, e] if p == 0 else real_current[p - 1][e]
            target = low_rim[p][e] if kind == RAW_UP else high_rim[p][e]
        elif kind == RAW_NEXT or kind == RAW_PREV:
            source = green.at[1, 0, e] if p == 0 else imag_source[p][e].at[1]
            target = imag_source[p][e].at[2 if kind == RAW_NEXT else 0]
        elif kind == SHARE_NEXT or kind == SHARE_PREV:
            way = 1 if kind == SHARE_NEXT else 0
            source, target = share_out[p].at[way, e], share_in[p].at[way, e]
        else:
            way = 1 if kind == PART_UP else 0
            source, target = part_out[p].at[way, e], part_in[p].at[way, e]
        if kind in (RAW_NEXT, SHARE_NEXT):
            device = {"mom": next_k}
        elif kind in (RAW_PREV, SHARE_PREV):
            device = {"mom": prev_k}
        elif kind in (RAW_UP, PART_UP):
            device = {"en": up_z}
        else:
            device = {"en": down_z}
        return pltpu.make_async_remote_copy(
            src_ref=source,
            dst_ref=target,
            send_sem=send_sem.at[p, kind, e],
            recv_sem=recv_sem.at[p, kind, e],
            device_id=device,
            device_id_type=pl.DeviceIdType.MESH,
        )

    def guarded(condition, action):
        if condition is None:
            action()
        else:
            pl.when(condition)(action)

    def sends_if(kind):
        return {RAW_UP: has_up, PART_UP: has_up, RAW_DOWN: has_down, PART_DOWN: has_down}.get(kind)

    def receives_if(kind):
        return {RAW_UP: has_down, PART_UP: has_down, RAW_DOWN: has_up, PART_DOWN: has_up}.get(kind)

    def start(p, kind, e):
        guarded(sends_if(kind), lambda: copy_of(p, kind, e).start())

    waited = set()

    def arrived(p, kind, e):
        if (p, kind, e) not in waited:
            waited.add((p, kind, e))
            guarded(receives_if(kind), lambda: copy_of(p, kind, e).wait_recv())

    order = []
    for i in range((energies + 1) // 2):
        order.append(i)
        if energies - 1 - i != i:
            order.append(energies - 1 - i)

    for e in order:
        start(0, RAW_NEXT, e)
        start(0, RAW_PREV, e)
        start(0, RAW_UP, e)
        start(0, RAW_DOWN, e)

    @pl.when(jnp.logical_not(has_down))
    def _():
        for p in range(passes):
            for e in range(energies):
                low_rim[p][e][...] = jnp.zeros_like(low_rim[p][e])
            part_in[p][1] = jnp.zeros_like(part_in[p][1])

    @pl.when(jnp.logical_not(has_up))
    def _():
        for p in range(passes):
            for e in range(energies):
                high_rim[p][e][...] = jnp.zeros_like(high_rim[p][e])
            part_in[p][0] = jnp.zeros_like(part_in[p][0])

    weight, shift, picks = [], [], []
    for m in range(MODES):
        mode = jnp.int32(0)
        for j in range(1, MODES):
            mode = jnp.where(mode_offset[j] == m + 1, jnp.int32(j), mode)
        weight.append(occupation[mode])
        shift.append(mode_shift[mode])
        picks.append([mode_block[b, mode] for b in range(blocks)])
        matrix = coupling[mode]
        matrices[m] = matrix
        matrices_t[pl.ds(m * size, size), :] = matrix.astype(f32).T.astype(bf16)
    slot_of = []
    for q in (-1, 0, 1):
        slot = jnp.int32(0)
        for m in range(1, MODES):
            slot = jnp.where(shift[m] == q, jnp.int32(m), slot)
        slot_of.append(slot)
    extra = sum(range(MODES)) - slot_of[0] - slot_of[1] - slot_of[2]
    extra_shift = jnp.int32(0)
    for m in range(MODES):
        extra_shift = jnp.where(extra == m, shift[m], extra_shift)
    extra_t = matrices[extra].astype(f32).T
    for q in range(3):
        pair_t[q, pl.ds(0, size), :] = matrices[slot_of[q]].astype(f32).T.astype(bf16)
        kept = jnp.where(extra_shift == q - 1, 1.0, 0.0).astype(f32)
        pair_t[q, pl.ds(size, size), :] = (extra_t * kept).astype(bf16)

    for e in range(energies):
        for b in range(blocks):
            real, imag = bare[0, 0, e, b], bare[1, 0, e, b]
            wide_bare[e, b, pl.ds(0, size), :] = side_by_side(real, imag)
            wide_bare[e, b, pl.ds(size, size), :] = side_by_side(-imag, real)
        imag_source[0][e][1] = green[1, 0, e]

    def real_at(p, e, pick):
        if e < 0:
            return low_rim[p][e + energies][pick]
        if e >= energies:
            return high_rim[p][e - energies][pick]
        return green[0, 0, e, pick] if p == 0 else real_current[p - 1][e][pick]

    def imag_step(p, e):
        arrived(p, RAW_NEXT, e)
        arrived(p, RAW_PREV, e)
        for m in range(MODES):
            chosen = imag_source[p][e][shift[m] + 1]
            coupled = matmul(matrices[m], side_by_side(*[chosen[c] for c in range(blocks)]))
            lower = (weight[m] * coupled).astype(bf16)
            upper = ((weight[m] + 1.0) * coupled).astype(bf16)
            for c in range(blocks):
                below[e, m, c] = lower[:, c * size:(c + 1) * size]
                above[e, m, c] = upper[:, c * size:(c + 1) * size]

    def part_of(target):
        lower = [m for m in range(MODES) if 0 <= target - m - 1 < energies]
        upper = [m for m in range(MODES) if 0 <= target + m + 1 < energies]
        rows = []
        for b in range(blocks):
            terms = [below[target - m - 1, m, picks[m][b]] for m in lower]
            terms += [above[target + m + 1, m, picks[m][b]] for m in upper]
            rows.append(side_by_side(*terms))
        spans = [
            matrices_t[pl.ds(ms[0] * size, len(ms) * size), :] for ms in (lower, upper) if ms
        ]
        return matmul(on_top(*rows), on_top(*spans))

    def send_part(p, way, e):
        target = e + energies if way == 1 else e - energies
        part = part_of(target).astype(bf16)
        for b in range(blocks):
            part_out[p][way, e, b] = part[b * size:(b + 1) * size]
        start(p, PART_UP if way == 1 else PART_DOWN, e)

    def real_step(p, e):
        for m in range(MODES):
            for at in (e - m - 1, e + m + 1):
                if at < 0:
                    arrived(p, RAW_UP, at + energies)
                elif at >= energies:
                    arrived(p, RAW_DOWN, at - energies)
        for m in range(MODES):
            summed = []
            for b in range(blocks):
                low_side = real_at(p, e - m - 1, picks[m][b]).astype(f32)
                high_side = real_at(p, e + m + 1, picks[m][b]).astype(f32)
                mixed = weight[m] * low_side + (weight[m] + 1.0) * high_side
                summed.append(mixed.astype(bf16))
            coupled = matmul(matrices[m], side_by_side(*summed)).astype(bf16)
            for b in range(blocks):
                real_coupled[e, m, pl.ds(b * size, size), :] = coupled[:, b * size:(b + 1) * size]
        rest = real_coupled[e, extra]
        for q in (0, 2, 1):
            share = matmul(side_by_side(real_coupled[e, slot_of[q]], rest), pair_t[q])
            if q == 1:
                share_own[e] = share
            else:
                rounded = share.astype(bf16)
                way = 1 if q == 2 else 0
                for b in range(blocks):
                    share_out[p][way, e, b] = rounded[b * size:(b + 1) * size]
                start(p, SHARE_NEXT if way == 1 else SHARE_PREV, e)

    def close_step(p, e):
        for kind in (SHARE_NEXT, SHARE_PREV, PART_UP, PART_DOWN):
            arrived(p, kind, e)
        for b in range(blocks):
            rows = slice(b * size, (b + 1) * size)
            real = share_own[e, rows] + share_in[p][0, e, b].astype(f32)
            real = (real + share_in[p][1, e, b].astype(f32)).astype(bf16)
            imag = part_own[e, rows] + part_in[p][0, e, b].astype(f32)
            imag = (imag + part_in[p][1, e, b].astype(f32)).astype(bf16)
            sigma = on_top(side_by_side(real, imag), side_by_side(-imag, real))
            both = wide_bare[e, b, pl.ds(0, size), :]
            product = matmul(both, sigma).astype(bf16)
            new = (both.astype(f32) + matmul(product, wide_bare[e, b])).astype(bf16)
            if p == passes - 1:
                out[0, 0, e, b] = new[:, :size]
                out[1, 0, e, b] = new[:, size:]
            else:
                real_current[p][e][b] = new[:, :size]
                imag_source[p + 1][e][1, b] = new[:, size:]
        if p < passes - 1:
            start(p + 1, RAW_NEXT, e)
            start(p + 1, RAW_PREV, e)
            start(p + 1, RAW_UP, e)
            start(p + 1, RAW_DOWN, e)

    for p in range(passes):
        done = set()
        todo = []
        for e in order:
            imag_step(p, e)
            done.add(e)
            if len(done) < energies:
                if all(i in done for i in range(e + 1)):
                    send_part(p, 0, e)
                    todo.append((0, e))
                if all(i in done for i in range(e, energies)):
                    send_part(p, 1, e)
                    todo.append((1, e))
        rest = [
            (way, e)
            for i in range(energies)
            for way, e in ((0, i), (1, energies - 1 - i))
            if (way, e) not in todo
        ]
        inner = order[::-1]
        for i in range(energies):
            real_step(p, inner[i])
            share_of = rest[i * len(rest) // energies:(i + 1) * len(rest) // energies]
            for way, e in share_of:
                send_part(p, way, e)
        for e in order:
            part_own[e] = part_of(e)
        for e in inner:
            close_step(p, e)

    for p in range(passes):
        for kind in range(KINDS):
            def finish(p=p, kind=kind):
                for e in range(energies):
                    copy_of(p, kind, e).wait_send()

            guarded(sends_if(kind), finish)


def shards(mom_count, en_count, green, bare, coupling, occupation, mode_shift, mode_offset, mode_block):
    _, _, energies, blocks, size, _ = green.shape
    assert energies == REACH and coupling.shape[0] == MODES and MODES == REACH
    pair = (blocks, size, size)
    vmem = pltpu.VMEM
    scratch = [
        vmem((MODES, size, size), bf16),
        vmem((MODES * size, size), bf16),
        vmem((3, 2 * size, size), bf16),
        vmem((energies, blocks, 2 * size, 2 * size), bf16),
        vmem((energies, MODES, blocks * size, size), bf16),
        vmem((energies, MODES) + pair, bf16),
        vmem((energies, MODES) + pair, bf16),
        vmem((energies, blocks * size, size), f32),
        vmem((energies, blocks * size, size), f32),
        [[vmem(pair, bf16) for _ in range(energies)] for _ in range(PASSES - 1)],
        [[vmem(pair, bf16) for _ in range(energies)] for _ in range(PASSES)],
        [[vmem(pair, bf16) for _ in range(energies)] for _ in range(PASSES)],
        [[vmem((3,) + pair, bf16) for _ in range(energies)] for _ in range(PASSES)],
        [vmem((2, energies) + pair, bf16) for _ in range(PASSES)],
        [vmem((2, energies) + pair, bf16) for _ in range(PASSES)],
        [vmem((2, energies) + pair, bf16) for _ in range(PASSES)],
        [vmem((2, energies) + pair, bf16) for _ in range(PASSES)],
        pltpu.SemaphoreType.DMA((PASSES, KINDS, energies)),
        pltpu.SemaphoreType.DMA((PASSES, KINDS, energies)),
    ]
    whole = pl.BlockSpec(memory_space=pltpu.VMEM)
    scalars = pl.BlockSpec(memory_space=pltpu.SMEM)
    return pl.pallas_call(
        functools.partial(kernel, mom_count, en_count, PASSES),
        out_shape=jax.ShapeDtypeStruct(green.shape, green.dtype),
        in_specs=[scalars] * 4 + [whole] * 3,
        out_specs=whole,
        scratch_shapes=scratch,
        compiler_params=pltpu.CompilerParams(
            collective_id=0, has_side_effects=True, vmem_limit_bytes=48 * 1024 * 1024
        ),
        name="born_passes",
    )(occupation, mode_shift, mode_offset, mode_block, green, bare, coupling)


def solution(mesh):
    spread = P(None, "mom", "en", None, None, None)
    return jax.shard_map(
        functools.partial(shards, mesh.shape["mom"], mesh.shape["en"]),
        mesh=mesh,
        in_specs=(spread, spread, P(), P(), P(), P(), P()),
        out_specs=spread,
        check_vma=False,
    )
```

time: 149 us -> 43.7 us (0.29)
  Pallas kernels: 0 us -> 37 us
  waiting for transfers between devices: 36.3 us -> 0 us
  between operations: 33.2 us -> 0.02 us
  local copies, waits for them, and re-layouts: 28 us -> 6.42 us
  matrix products: 17.2 us -> 0 us
  starting transfers between devices: 17.1 us -> 0 us
  other arithmetic: 16.3 us -> 0 us
    pallas_call x0 -> x1, Pallas kernels: none -> 37 us  [shards(): pl.pallas_call(functools.partial(kernel, mom_count, en_count, PASSES), ou...]
    ppermute x8 -> x0, waiting for transfers between devices: 36.3 us -> none  [the longest x4 27.5 us: shifted(): lax.ppermute(array, axis, [(i, (i + by) % size) for i in range(size)])]
    dot_general x24 -> x0, matrix products: 17.2 us -> none  [the longest x8 12.6 us: mode_term(): jnp.einsum('...ab,cb->...ac', coupled, matrix, preferred_element_type=jnp...]
    ppermute x8 -> x0, starting transfers between devices: 17.1 us -> none  [the longest x2 10.4 us: extended(): lax.ppermute(lax.slice_in_dim(block, block.shape[dim] - width, None, axis...]
    convert_element_type x8 -> x0, other arithmetic: 11.6 us -> none  [the longest x4 8.51 us: mode_term(): pieces.append(mixed.astype(jnp.bfloat16))]
    dynamic_slice x9 -> x0, local copies, waits for them, and re-layouts: 9.74 us -> none  [shares_by_shift(): previous = lax.dynamic_index_in_dim(shares, which, 0, keepdims=False)]
    slice x4 -> x0, local copies, waits for them, and re-layouts: 6.03 us -> none  [the longest x1 1.64 us: mode_term(): mode_block[target, mode_index]]
    unnamed x10 -> x15, local copies, waits for them, and re-layouts: 1.61 us -> 6.42 us
  transfers between devices with their start and end apart: 8 -> 0, of which waited for: 6 -> 0; matrix products, arithmetic and copies ran while one was open for 4% -> 0% of each run, Pallas kernels for 0% -> 0%
where the time goes in v1:
time: 43.7 us; the launch traced here: 43.5 us
  Pallas kernels  37 us (85%)
  local copies, waits for them, and re-layouts  6.42 us (15%)
    pallas_call x1, Pallas kernels, shards(): pl.pallas_call(functools.partial(kernel, mom_count, en_count, PASSES), ou...  37 us
    unnamed x15, local copies, waits for them, and re-layouts  6.42 us

profile of v1, /device:TPU:0, one launch (start us, length us, event | category | flops | bytes accessed | tf_op | source)
XLA Modules:
  0.0 43.5 jit_solution(18183198934436350667)
XLA Ops:
  0.0 0.0 copy-start
  0.0 1.0 %copy-done = bf16[2,1,4,2,128,128]{5,4,3,2,1,0:T(8,128)(2,1)S(1)} copy-done((bf16[2,1,4,2,128,128]{5,4,3,2,1,0:T(8,128)(2,1)S(1)}, bf16[2,1,4,2,128,128]{5,4,3,2,1,0:T(8,128)(2,1)}, u32[]{:S(2)}) %copy-start) | copy-done | bytes 524312
  1.0 0.0 copy-start.1
  1.0 1.0 %copy-done.1 = bf16[2,1,4,2,128,128]{5,4,3,2,1,0:T(8,128)(2,1)S(1)} copy-done((bf16[2,1,4,2,128,128]{5,4,3,2,1,0:T(8,128)(2,1)S(1)}, bf16[2,1,4,2,128,128]{5,4,3,2,1,0:T(8,128)(2,1)}, u32[]{:S(2)}) %copy-start.1) | copy-done | bytes 524312
  2.1 0.0 copy-start.2
  2.1 0.9 %copy-done.2 = bf16[4,128,128]{2,1,0:T(8,128)(2,1)S(1)} copy-done((bf16[4,128,128]{2,1,0:T(8,128)(2,1)S(1)}, bf16[4,128,128]{2,1,0:T(8,128)(2,1)}, u32[]{:S(2)}) %copy-start.2) | copy-done | bytes 131096
  3.0 0.0 copy-start.3
  3.0 0.7 %copy-done.3 = s32[2,4]{1,0:T(2,128)S(1)} copy-done((s32[2,4]{1,0:T(2,128)S(1)}, s32[2,4]{1,0:T(2,128)}, u32[]{:S(2)}) %copy-start.3) | copy-done | bytes 56
  3.7 0.0 copy-start.4
  3.7 0.7 %copy-done.4 = f32[4]{0:T(128)S(1)} copy-done((f32[4]{0:T(128)S(1)}, f32[4]{0:T(128)}, u32[]{:S(2)}) %copy-start.4) | copy-done | bytes 40
  4.3 0.0 copy-start.5
  4.3 0.7 %copy-done.5 = s32[4]{0:T(128)S(1)} copy-done((s32[4]{0:T(128)S(1)}, s32[4]{0:T(128)}, u32[]{:S(2)}) %copy-start.5) | copy-done | bytes 40
  5.0 0.0 copy-start.6
  5.0 0.7 %copy-done.6 = s32[4]{0:T(128)S(1)} copy-done((s32[4]{0:T(128)S(1)}, s32[4]{0:T(128)}, u32[]{:S(2)}) %copy-start.6) | copy-done | bytes 40
  5.6 37.0 %born_passes.1 = bf16[2,1,4,2,128,128]{5,4,3,2,1,0:T(8,128)(2,1)S(1)} custom-call(f32[4]{0:T(128)S(1)} %copy-done.4, s32[4]{0:T(128)S(1)} %copy-done.5, s32[4]{0:T(128)S(1)} %copy-done.6, s32[2,4]{1,0:T(2,128)S(1)} %copy-done.3, bf16[2,1,4,2,128,128]{5,4,3,2,1,0:T(8,128)(2,1)S(1)} %copy-done, bf16[2,1,4,2,128,128]{5,4,3,2,1,0:T(8,128)(2,1)S(1)} %copy-done.1, ...), custom_call_target="tpu_custom_call" | custom-call | tf_op jit(solution)/shard_map/born_passes/pallas_call | solution.py:345
  42.7 0.8 %copy.9 = bf16[2,1,4,2,128,128]{5,4,3,2,1,0:T(8,128)(2,1)} copy(bf16[2,1,4,2,128,128]{5,4,3,2,1,0:T(8,128)(2,1)S(1)} %born_passes.1) | data formatting | bytes 1048576
Async XLA Ops:
  0.0 1.0 %copy-start = (bf16[2,1,4,2,128,128]{5,4,3,2,1,0:T(8,128)(2,1)S(1)}, bf16[2,1,4,2,128,128]{5,4,3,2,1,0:T(8,128)(2,1)}, u32[]{:S(2)}) copy-start(bf16[2,1,4,2,128,128]{5,4,3,2,1,0:T(8,128)(2,1)} %green.1) | copy-start | bytes 1572868
  1.0 1.0 %copy-start.1 = (bf16[2,1,4,2,128,128]{5,4,3,2,1,0:T(8,128)(2,1)S(1)}, bf16[2,1,4,2,128,128]{5,4,3,2,1,0:T(8,128)(2,1)}, u32[]{:S(2)}) copy-start(bf16[2,1,4,2,128,128]{5,4,3,2,1,0:T(8,128)(2,1)} %bare.1) | copy-start | bytes 1572868
  2.1 0.9 %copy-start.2 = (bf16[4,128,128]{2,1,0:T(8,128)(2,1)S(1)}, bf16[4,128,128]{2,1,0:T(8,128)(2,1)}, u32[]{:S(2)}) copy-start(bf16[4,128,128]{2,1,0:T(8,128)(2,1)} %coupling.1) | copy-start | bytes 393220
  3.0 0.7 %copy-start.3 = (s32[2,4]{1,0:T(2,128)S(1)}, s32[2,4]{1,0:T(2,128)}, u32[]{:S(2)}) copy-start(s32[2,4]{1,0:T(2,128)} %mode_block.1) | copy-start | bytes 100
  3.7 0.7 %copy-start.4 = (f32[4]{0:T(128)S(1)}, f32[4]{0:T(128)}, u32[]{:S(2)}) copy-start(f32[4]{0:T(128)} %occupation.1) | copy-start | bytes 52
  4.3 0.7 %copy-start.5 = (s32[4]{0:T(128)S(1)}, s32[4]{0:T(128)}, u32[]{:S(2)}) copy-start(s32[4]{0:T(128)} %mode_shift.1) | copy-start | bytes 52
  5.0 0.7 %copy-start.6 = (s32[4]{0:T(128)S(1)}, s32[4]{0:T(128)}, u32[]{:S(2)}) copy-start(s32[4]{0:T(128)} %mode_offset.1) | copy-start | bytes 52

commit v2 on v1

--- a/solution.py
+++ b/solution.py
@@ -32,11 +32,12 @@
 
 def kernel(
     mom_count, en_count, passes,
-    occupation, mode_shift, mode_offset, mode_block, green, bare, coupling,
+    occupation_hbm, mode_shift_hbm, mode_offset_hbm, mode_block_hbm, green, bare_hbm, coupling_hbm,
     out,
+    occupation, mode_shift, mode_offset, mode_block, bare, coupling, first_real,
     matrices, matrices_t, pair_t, wide_bare, real_coupled, below, above,
     share_own, part_own, real_current, low_rim, high_rim, imag_source,
-    share_out, share_in, part_out, part_in, send_sem, recv_sem,
+    share_out, share_in, part_out, part_in, send_sem, recv_sem, green_sem, input_sem,
 ):
     energies = green.shape[2]
     blocks = green.shape[3]
@@ -68,14 +69,44 @@
             barrier, inc=1, device_id={"en": down_z}, device_id_type=pl.DeviceIdType.MESH
         )
 
+    middle = list(range(1, energies - 1))
+    ends = [0, energies - 1]
+    upward = list(range(energies))[::-1]
+    downward = list(range(energies))
+
+    real_fetch = [
+        pltpu.make_async_copy(green.at[0, 0, e], first_real[e], green_sem.at[0, e])
+        for e in range(energies)
+    ]
+    imag_fetch = [
+        pltpu.make_async_copy(green.at[1, 0, e], imag_source[0][e].at[1], green_sem.at[1, e])
+        for e in range(energies)
+    ]
+    pairs = (
+        (coupling_hbm, coupling),
+        (bare_hbm, bare),
+        (occupation_hbm, occupation),
+        (mode_shift_hbm, mode_shift),
+        (mode_offset_hbm, mode_offset),
+        (mode_block_hbm, mode_block),
+    )
+    input_fetch = [
+        pltpu.make_async_copy(there, here, input_sem.at[i]) for i, (there, here) in enumerate(pairs)
+    ]
+    for e in ends + middle:
+        imag_fetch[e].start()
+        real_fetch[e].start()
+    for fetch in input_fetch:
+        fetch.start()
+
     pl.semaphore_wait(barrier, 2 + has_up.astype(jnp.int32) + has_down.astype(jnp.int32))
 
     def copy_of(p, kind, e):
         if kind == RAW_UP or kind == RAW_DOWN:
-            source = green.at[0, 0, e] if p == 0 else real_current[p - 1][e]
+            source = first_real[e] if p == 0 else real_current[p - 1][e]
             target = low_rim[p][e] if kind == RAW_UP else high_rim[p][e]
         elif kind == RAW_NEXT or kind == RAW_PREV:
-            source = green.at[1, 0, e] if p == 0 else imag_source[p][e].at[1]
+            source = imag_source[p][e].at[1]
             target = imag_source[p][e].at[2 if kind == RAW_NEXT else 0]
         elif kind == SHARE_NEXT or kind == SHARE_PREV:
             way = 1 if kind == SHARE_NEXT else 0
@@ -122,17 +153,15 @@
             waited.add((p, kind, e))
             guarded(receives_if(kind), lambda: copy_of(p, kind, e).wait_recv())
 
-    order = []
-    for i in range((energies + 1) // 2):
-        order.append(i)
-        if energies - 1 - i != i:
-            order.append(energies - 1 - i)
-
-    for e in order:
+    for i, e in enumerate(ends + middle):
+        imag_fetch[e].wait()
         start(0, RAW_NEXT, e)
         start(0, RAW_PREV, e)
-        start(0, RAW_UP, e)
-        start(0, RAW_DOWN, e)
+    for fetch in real_fetch:
+        fetch.wait()
+    for i in range(energies):
+        start(0, RAW_UP, upward[i])
+        start(0, RAW_DOWN, downward[i])
 
     @pl.when(jnp.logical_not(has_down))
     def _():
@@ -147,6 +176,9 @@
             for e in range(energies):
                 high_rim[p][e][...] = jnp.zeros_like(high_rim[p][e])
             part_in[p][0] = jnp.zeros_like(part_in[p][0])
+
+    for fetch in input_fetch:
+        fetch.wait()
 
     weight, shift, picks = [], [], []
     for m in range(MODES):
@@ -180,14 +212,13 @@
             real, imag = bare[0, 0, e, b], bare[1, 0, e, b]
             wide_bare[e, b, pl.ds(0, size), :] = side_by_side(real, imag)
             wide_bare[e, b, pl.ds(size, size), :] = side_by_side(-imag, real)
-        imag_source[0][e][1] = green[1, 0, e]
 
     def real_at(p, e, pick):
         if e < 0:
             return low_rim[p][e + energies][pick]
         if e >= energies:
             return high_rim[p][e - energies][pick]
-        return green[0, 0, e, pick] if p == 0 else real_current[p - 1][e][pick]
+        return first_real[e][pick] if p == 0 else real_current[p - 1][e][pick]
 
     def imag_step(p, e):
         arrived(p, RAW_NEXT, e)
@@ -276,33 +307,41 @@
             start(p + 1, RAW_DOWN, e)
 
     for p in range(passes):
-        done = set()
-        todo = []
-        for e in order:
+        imag_order = ends + middle if p == 0 else middle + ends
+        share_order = middle + ends
+        shares, done, sent = list(share_order), set(), set()
+
+        def ready_parts():
+            found = []
+            for i in range(energies):
+                if all(j in done for j in range(i + 1)):
+                    found.append((0, i))
+                if all(j in done for j in range(energies - 1 - i, energies)):
+                    found.append((1, energies - 1 - i))
+            return [item for item in found if item not in sent]
+
+        def send_next_part():
+            way_and_energy = ready_parts()[0]
+            sent.add(way_and_energy)
+            send_part(p, *way_and_energy)
+
+        for e in imag_order:
+            if p == 0 and e == imag_order[-1]:
+                for _ in middle:
+                    real_step(p, shares.pop(0))
             imag_step(p, e)
             done.add(e)
             if len(done) < energies:
-                if all(i in done for i in range(e + 1)):
-                    send_part(p, 0, e)
-                    todo.append((0, e))
-                if all(i in done for i in range(e, energies)):
-                    send_part(p, 1, e)
-                    todo.append((1, e))
-        rest = [
-            (way, e)
-            for i in range(energies)
-            for way, e in ((0, i), (1, energies - 1 - i))
-            if (way, e) not in todo
-        ]
-        inner = order[::-1]
-        for i in range(energies):
-            real_step(p, inner[i])
-            share_of = rest[i * len(rest) // energies:(i + 1) * len(rest) // energies]
-            for way, e in share_of:
-                send_part(p, way, e)
-        for e in order:
+                while ready_parts():
+                    send_next_part()
+        while ready_parts() or shares:
+            if ready_parts():
+                send_next_part()
+            if shares and not (p == 0 and len(ready_parts()) % 2):
+                real_step(p, shares.pop(0))
+        for e in share_order:
             part_own[e] = part_of(e)
-        for e in inner:
+        for e in share_order:
             close_step(p, e)
 
     for p in range(passes):
@@ -319,7 +358,15 @@
     assert energies == REACH and coupling.shape[0] == MODES and MODES == REACH
     pair = (blocks, size, size)
     vmem = pltpu.VMEM
+    smem = pltpu.SMEM
     scratch = [
+        smem(occupation.shape, occupation.dtype),
+        smem(mode_shift.shape, mode_shift.dtype),
+        smem(mode_offset.shape, mode_offset.dtype),
+        smem(mode_block.shape, mode_block.dtype),
+        vmem(bare.shape, bf16),
+        vmem(coupling.shape, bf16),
+        [vmem(pair, bf16) for _ in range(energies)],
         vmem((MODES, size, size), bf16),
         vmem((MODES * size, size), bf16),
         vmem((3, 2 * size, size), bf16),
@@ -339,18 +386,18 @@
         [vmem((2, energies) + pair, bf16) for _ in range(PASSES)],
         pltpu.SemaphoreType.DMA((PASSES, KINDS, energies)),
         pltpu.SemaphoreType.DMA((PASSES, KINDS, energies)),
+        pltpu.SemaphoreType.DMA((2, energies)),
+        pltpu.SemaphoreType.DMA((6,)),
     ]
     whole = pl.BlockSpec(memory_space=pltpu.VMEM)
-    scalars = pl.BlockSpec(memory_space=pltpu.SMEM)
+    anywhere = pl.BlockSpec(memory_space=pl.ANY)
     return pl.pallas_call(
         functools.partial(kernel, mom_count, en_count, PASSES),
         out_shape=jax.ShapeDtypeStruct(green.shape, green.dtype),
-        in_specs=[scalars] * 4 + [whole] * 3,
+        in_specs=[anywhere] * 7,
         out_specs=whole,
         scratch_shapes=scratch,
-        compiler_params=pltpu.CompilerParams(
-            collective_id=0, has_side_effects=True, vmem_limit_bytes=48 * 1024 * 1024
-        ),
+        compiler_params=pltpu.CompilerParams(collective_id=0, has_side_effects=True),
         name="born_passes",
     )(occupation, mode_shift, mode_offset, mode_block, green, bare, coupling)
 

time: 43.7 us -> 37.1 us (0.85)
  local copies, waits for them, and re-layouts: 6.42 us -> 1.89 us
  Pallas kernels: 37 us -> 35 us
    unnamed x15 -> x1, local copies, waits for them, and re-layouts: 6.42 us -> 1.89 us
    pallas_call x1, Pallas kernels: 37 us -> 35 us  [shards(): pl.pallas_call(functools.partial(kernel, mom_count, en_count, PASSES), ou...]
where the time goes in v2:
time: 37.1 us; the launch traced here: 36.9 us
  Pallas kernels  35 us (94%)
  local copies, waits for them, and re-layouts  1.89 us (5%)
    pallas_call x1, Pallas kernels, shards(): pl.pallas_call(functools.partial(kernel, mom_count, en_count, PASSES), ou...  35 us
    unnamed x1, local copies, waits for them, and re-layouts  1.89 us

profile of v2, /device:TPU:0, one launch (start us, length us, event | category | flops | bytes accessed | tf_op | source)
XLA Modules:
  0.0 36.9 jit_solution(6415569644237705633)
XLA Ops:
  0.0 35.0 %born_passes.1 = bf16[2,1,4,2,128,128]{5,4,3,2,1,0:T(8,128)(2,1)} custom-call(f32[4]{0:T(128)} %occupation_hbm.1, s32[4]{0:T(128)} %mode_shift_hbm.1, s32[4]{0:T(128)} %mode_offset_hbm.1, s32[2,4]{1,0:T(2,128)} %mode_block_hbm.1, bf16[2,1,4,2,128,128]{5,4,3,2,1,0:T(8,128)(2,1)} %green.1, bf16[2,1,4,2,128,128]{5,4,3,2,1,0:T(8,128)(2,1)} %bare_hbm.1, ...), custom_call_target="tpu_custom_call" | custom-call | tf_op jit(solution)/shard_map/born_passes/pallas_call | solution.py:394
  35.0 1.9 %copy.9 = bf16[2,1,4,2,128,128]{5,4,3,2,1,0:T(8,128)(2,1)} copy(bf16[2,1,4,2,128,128]{5,4,3,2,1,0:T(8,128)(2,1)} %born_passes.1) | data formatting | bytes 1048576

commit v3 on v2

--- a/solution.py
+++ b/solution.py
@@ -326,7 +326,7 @@
             send_part(p, *way_and_energy)
 
         for e in imag_order:
-            if p == 0 and e == imag_order[-1]:
+            if (p == 0 and e == imag_order[len(ends)]) or (p > 0 and e == imag_order[-1]):
                 for _ in middle:
                     real_step(p, shares.pop(0))
             imag_step(p, e)
@@ -337,7 +337,7 @@
         while ready_parts() or shares:
             if ready_parts():
                 send_next_part()
-            if shares and not (p == 0 and len(ready_parts()) % 2):
+            if shares and len(ready_parts()) % 2 == 0:
                 real_step(p, shares.pop(0))
         for e in share_order:
             part_own[e] = part_of(e)
@@ -390,16 +390,18 @@
         pltpu.SemaphoreType.DMA((6,)),
     ]
     whole = pl.BlockSpec(memory_space=pltpu.VMEM)
-    anywhere = pl.BlockSpec(memory_space=pl.ANY)
+    anywhere = pl.BlockSpec(memory_space=pltpu.HBM)
     return pl.pallas_call(
         functools.partial(kernel, mom_count, en_count, PASSES),
         out_shape=jax.ShapeDtypeStruct(green.shape, green.dtype),
         in_specs=[anywhere] * 7,
         out_specs=whole,
         scratch_shapes=scratch,
-        compiler_params=pltpu.CompilerParams(collective_id=0, has_side_effects=True),
+        compiler_params=pltpu.CompilerParams(
+            collective_id=0, has_side_effects=True, vmem_limit_bytes=40 * 1024 * 1024
+        ),
         name="born_passes",
-    )(occupation, mode_shift, mode_offset, mode_block, green, bare, coupling)
+    )(*[pltpu.with_memory_space_constraint(a, pltpu.HBM) for a in (occupation, mode_shift, mode_offset, mode_block, green, bare, coupling)])
 
 
 def solution(mesh):

time: 37.1 us -> 35 us (0.943)
  local copies, waits for them, and re-layouts: 1.89 us -> 0.8 us
  Pallas kernels: 35 us -> 34 us
    unnamed x1, local copies, waits for them, and re-layouts: 1.89 us -> 0.8 us
    pallas_call x1, Pallas kernels: 35 us -> 34 us  [shards(): pl.pallas_call(functools.partial(kernel, mom_count, en_count, PASSES), ou...]
where the time goes in v3:
time: 35 us; the launch traced here: 34.8 us
  Pallas kernels  34 us (97%)
  local copies, waits for them, and re-layouts  0.8 us (2%)
    pallas_call x1, Pallas kernels, shards(): pl.pallas_call(functools.partial(kernel, mom_count, en_count, PASSES), ou...  34 us
    unnamed x1, local copies, waits for them, and re-layouts  0.8 us

profile of v3, /device:TPU:0, one launch (start us, length us, event | category | flops | bytes accessed | tf_op | source)
XLA Modules:
  0.0 34.8 jit_solution(7677456915687511336)
XLA Ops:
  0.0 34.0 %born_passes.1 = bf16[2,1,4,2,128,128]{5,4,3,2,1,0:T(8,128)(2,1)S(1)} custom-call(f32[4]{0:T(128)} %occupation_hbm.1, s32[4]{0:T(128)} %mode_shift_hbm.1, s32[4]{0:T(128)} %mode_offset_hbm.1, s32[2,4]{1,0:T(2,128)} %mode_block_hbm.1, bf16[2,1,4,2,128,128]{5,4,3,2,1,0:T(8,128)(2,1)} %green.1, bf16[2,1,4,2,128,128]{5,4,3,2,1,0:T(8,128)(2,1)} %bare_hbm.1, ...), custom_call_target="tpu_custom_call" | custom-call | tf_op jit(solution)/shard_map/born_passes/pallas_call | solution.py:394
  34.0 0.8 %copy.9 = bf16[2,1,4,2,128,128]{5,4,3,2,1,0:T(8,128)(2,1)} copy(bf16[2,1,4,2,128,128]{5,4,3,2,1,0:T(8,128)(2,1)S(1)} %born_passes.1) | data formatting | bytes 1048576
